TPU v7x, 256 devices: a whole 4x4x8 slice. The times are simulated.
256 devices in a mesh: expert: 32 (over x, z_hi, core), tensor: 8 (over y, z_lo).
Axes of the slice: x: 4, y: 4, z: 8 (z_hi: 4, z_lo: 2; z = z_hi * 2 + z_lo), core: 2. Of those that a mesh axis runs over, the one named last changes fastest.
Arguments:
- tokens: bfloat16 [512, 7168], P('expert'), may hold values from -6 to 6
- routes: int32 [512, 8], P('expert'), may hold values from 0 to 31, all different within a row; in each aligned block of 16 rows (0 to 15, 16 to 31, ...) at most 8 rows name the same one
- route_logits: float32 [512, 8], P('expert'), may hold values from -8 to 8
- gate_weight: bfloat16 [32, 7168, 1024], P('expert', 'tensor'), may hold values from -0.0625 to 0.0625
- up_weight: bfloat16 [32, 7168, 1024], P('expert', 'tensor'), may hold values from -0.0625 to 0.0625
- down_weight: bfloat16 [32, 7168, 1024], P('expert', 'tensor'), may hold values from -0.1875 to 0.1875
Outputs:
- mixed: bfloat16 [512, 7168], P('expert', 'tensor')
Inputs may be any that keep to these rules, and one draw needn't show every extreme that they name: `routes`: each row names 8 different experts. In each aligned block of 16 rows (the rows of one index of expert) no expert is named by more than 8 rows, a bound that some block reaches.
All inputs are finite; a program needn't handle non-finite values.
Results may differ from a plain program's by a relative error of at most 0.0066.
Values may be sent and summed in bfloat16 or wider, within the bound.
No kernel may reach another device: no remote copies, remote signals or barrier semaphores. Data moves between devices by JAX's collectives and lax.ppermute only.
A program may use at most 64 MiB of HBM per device.

v0:
```python
import jax
import jax.numpy as jnp
from jax import lax
from jax.sharding import PartitionSpec as P

routed_scale = 2.5


def cut_along(array, dim, peers):
    shape = array.shape
    blocks = array.reshape(*shape[:dim], peers, shape[dim] // peers, *shape[dim + 1 :])
    return jnp.moveaxis(blocks, dim, 0)


def summed_on_arrival(array, axis, dim):
    blocks = cut_along(array, dim, lax.axis_size(axis))
    arrived = lax.all_to_all(blocks, axis, split_axis=0, concat_axis=0, tiled=True)
    return arrived.sum(axis=0)


def sent_together(arrays, axis, dim, along):
    both = jnp.concatenate(arrays, axis=along)
    filled, at, finished = (summed_on_arrival(both, axis, dim), 0, [])
    for a in arrays:
        finished.append(lax.slice_in_dim(filled, at, at + a.shape[along], axis=along))
        at += a.shape[along]
    return tuple(finished)


def copy_for_each(array, axis):
    copies = jnp.broadcast_to(array, (lax.axis_size(axis), *array.shape))
    return lax.all_to_all(copies, axis, split_axis=0, concat_axis=0, tiled=True)


def in_order(blocks, dim):
    blocks = jnp.moveaxis(blocks, 0, dim)
    shape = blocks.shape
    return blocks.reshape(*shape[:dim], shape[dim] * shape[dim + 1], *shape[dim + 2 :])


def gathered_copies(array, axis, dim):
    blocks = copy_for_each(array, axis)
    return in_order(blocks, dim)


def shards(tokens, routes, route_logits, gate_weight, up_weight, down_weight):
    group_count = lax.axis_size("expert")
    shard_count = lax.axis_size("tensor")
    tensor_rank = lax.axis_index("tensor")
    local_tokens, model_width = tokens.shape
    route_count = routes.shape[1]
    local_experts = gate_weight.shape[0]
    expert_count = local_experts * group_count
    capacity = local_tokens // 2
    slot_count = expert_count * capacity
    narrow_width = model_width // shard_count
    scores = jax.nn.sigmoid(route_logits)
    weights = routed_scale * scores / jnp.sum(scores, axis=1, keepdims=True)
    flat_routes = routes.reshape(-1)
    one_hot = (flat_routes[:, None] == jnp.arange(expert_count, dtype=jnp.int32)[None, :]).astype(
        jnp.int32
    )
    earlier = jnp.cumsum(one_hot, axis=0) - one_hot
    position = jnp.sum(earlier * one_hot, axis=1)
    target = flat_routes * capacity + position
    matches = (jnp.arange(slot_count, dtype=jnp.int32)[:, None] == target[None, :]).reshape(
        slot_count, local_tokens, route_count
    )
    selector = jnp.sum(matches.astype(jnp.float32), axis=2).astype(jnp.bfloat16)
    combiner = jnp.sum(jnp.where(matches, weights[None, :, :], 0.0), axis=2).T
    own_columns = lax.dynamic_slice_in_dim(tokens, tensor_rank * narrow_width, narrow_width, 1)
    send_rows = jnp.dot(selector, own_columns, preferred_element_type=jnp.float32).astype(
        jnp.bfloat16
    )
    send_rows = send_rows.reshape(expert_count, capacity, own_columns.shape[1])
    received = lax.all_to_all(send_rows, "expert", split_axis=0, concat_axis=1, tiled=True)
    gate_part = jnp.einsum(
        "erd,edf->erf", received, gate_weight, preferred_element_type=jnp.float32
    )
    up_part = jnp.einsum("erd,edf->erf", received, up_weight, preferred_element_type=jnp.float32)
    gate_value, up_value = sent_together((gate_part, up_part), "tensor", 2, 0)
    hidden_part = (jax.nn.silu(gate_value) * up_value).astype(jnp.bfloat16)
    hidden = gathered_copies(hidden_part, "tensor", 2)
    column_rows = jnp.einsum(
        "erf,edf->erd", hidden, down_weight, preferred_element_type=jnp.float32
    )
    returned = lax.all_to_all(
        column_rows.astype(jnp.bfloat16), "expert", split_axis=1, concat_axis=0, tiled=True
    ).astype(column_rows.dtype)
    mixed = jnp.dot(
        combiner,
        returned.reshape(slot_count, narrow_width),
        precision=lax.Precision.HIGHEST,
        preferred_element_type=jnp.float32,
    )
    return mixed.astype(jnp.bfloat16)


def solution(mesh):
    return jax.shard_map(
        shards,
        mesh=mesh,
        in_specs=(
            P("expert", None),
            P("expert", None),
            P("expert", None),
            P("expert", "tensor", None),
            P("expert", "tensor", None),
            P("expert", "tensor", None),
        ),
        out_specs=P("expert", "tensor"),
        check_vma=False,
    )
```

profile of v0, /device:TPU:1, one launch (start us, length us, event | category | flops | bytes accessed | tf_op | source)
XLA Modules:
  0.0 113.4 jit_solution(8549494154525282923)
XLA Ops:
  0.0 0.0 copy-start
  0.0 0.9 copy.37
  0.9 0.1 eq.30
  1.0 0.1 fusion.14
  1.1 0.2 reduce_window_sum.11
  1.3 0.2 select_reduce_fusion.1
  1.4 0.1 reduce_sum.48
  1.5 0.7 fusion.18
  2.2 0.7 multiply_divide_fusion
  3.0 0.1 copy.39
  3.0 0.2 convert_reduce_fusion
  3.2 1.8 %fusion.5 = bf16[32,8,896]{2,1,0:T(8,128)(2,1)} fusion(bf16[16,7168]{1,0:T(8,128)(2,1)} %param.6, s32[]{:T(128)S(6)} %select_n.8, bf16[256,16]{0,1:T(8,128)(2,1)S(1)} %get-tuple-element.5), kind=kOutput, calls=%fused_computation.7 | convolution fusion | flops 7569408 | bytes 495620 | tf_op jit(solution)/shard_map/dot_general | solution.py:72
  5.0 12.6 %all-to-all-start = ((bf16[32,8,896]{2,1,0:T(8,128)(2,1)}), bf16[32,8,896]{2,1,0:T(8,128)(2,1)S(1)}, u32[]{:S(2)}, u32[]{:S(2)}) async-start(bf16[32,8,896]{2,1,0:T(8,128)(2,1)} %fusion.5), calls=%async_computation | async-start | bytes 917504 | tf_op jit(solution)/shard_map/all_to_all | solution.py:76
  17.6 3.8 %copy.48 = bf16[1024,896]{1,0:T(8,128)(2,1)} copy(bf16[1024,896]{0,1:T(8,128)(2,1)} %bitcast.55) | data formatting | bytes 3670016 | tf_op jit(solution)/shard_map/erd,edf->erf/dot_general | solution.py:80
  21.5 3.8 %copy.47 = bf16[1024,896]{1,0:T(8,128)(2,1)} copy(bf16[1024,896]{0,1:T(8,128)(2,1)} %bitcast.56) | data formatting | bytes 3670016 | tf_op jit(solution)/shard_map/erd,edf->erf/dot_general | solution.py:77
  25.3 8.8 %all-to-all-done = bf16[32,8,896]{2,1,0:T(8,128)(2,1)S(1)} async-done(((bf16[32,8,896]{2,1,0:T(8,128)(2,1)}), bf16[32,8,896]{2,1,0:T(8,128)(2,1)S(1)}, u32[]{:S(2)}, u32[]{:S(2)}) %all-to-all-start) | async-done | bytes 458784 | tf_op jit(solution)/shard_map/all_to_all | solution.py:76
  34.0 0.0 copy-start.1
  34.0 2.4 %convolution_bitcast_fusion = f32[1,256,8,128]{3,1,2,0:T(8,128)S(1)} fusion(bf16[8,128,896]{2,1,0:T(8,128)(2,1)} %bitcast.52, bf16[32,8,896]{2,1,0:T(8,128)(2,1)S(1)} %all-to-all-done), kind=kOutput, calls=%fused_computation.3 | convolution fusion | flops 469762048 | bytes 3342336 | tf_op jit(solution)/shard_map/erd,edf->erf/dot_general | solution.py:80
  36.4 0.0 copy-done.1
  36.4 0.8 convolution_bitcast_fusion.1
  37.2 0.2 maximum_bitcast_fusion
  37.4 0.2 copy.42
  37.6 31.8 %all_to_all.28 = f32[8,2,256,128]{3,2,1,0:T(8,128)} all-to-all(f32[8,2,256,128]{3,2,1,0:T(8,128)S(1)} %copy.42), channel_id=1, replica_groups=mesh['expert'=32,'tensor'=8] {'tensor'}, dimensions={0} | all-to-all | bytes 4194304 | tf_op jit(solution)/shard_map/all_to_all | solution.py:17
  69.4 1.7 %reduce_sum.52 = f32[2,256,128]{2,1,0:T(8,128)S(1)} reduce(f32[8,2,256,128]{3,2,1,0:T(8,128)} %all_to_all.28, f32[]{:T(128)} %constant.6.clone.1), dimensions={0}, to_apply=%region_5.6 | reduce | flops 458752 | bytes 2359300 | tf_op jit(solution)/shard_map/reduce_sum | solution.py:18
  71.2 0.1 copy.44
  71.3 11.6 %all_to_all.29 = bf16[8,1,256,128]{2,3,1,0:T(8,128)(2,1)S(1)} all-to-all(bf16[8,1,256,128]{2,3,1,0:T(8,128)(2,1)S(1)} %broadcast_in_dim.22), channel_id=1, replica_groups=mesh['expert'=32,'tensor'=8] {'tensor'}, dimensions={0} | all-to-all | bytes 1048576 | tf_op jit(solution)/shard_map/all_to_all | solution.py:32
  83.0 0.0 copy-done
  83.0 0.8 fusion.6
  83.7 0.7 copy.58
  84.5 0.5 broadcast.28
  85.0 3.4 %reduce = bf16[256,896]{1,0:T(8,128)(2,1)S(1)} reduce(bf16[256,1,896]{2,1,0:T(2,128)(2,1)S(1)} %bitcast.53, bf16[]{:T(256)} %broadcast.28), dimensions={1}, to_apply=%bitcast.50.reduce_sub_computation | reduce | bytes 917506
  88.4 0.2 reshape.84
  88.6 23.5 %all_to_all.30 = bf16[32,2,3584]{2,1,0:T(2,128)(2,1)S(1)} all-to-all(bf16[32,2,3584]{2,1,0:T(2,128)(2,1)S(1)} %reshape.84), channel_id=1, replica_groups=mesh['expert'=32,'tensor'=8] {'expert'}, dimensions={0} | all-to-all | bytes 917504 | tf_op jit(solution)/shard_map/all_to_all | solution.py:87
  112.1 0.4 reshape.85
  112.5 0.9 convolution_convert_fusion.1
  (3 shorter events, 0.1 us)
Async XLA Ops:
  0.0 83.0 %copy-start = (bf16[1,896,1024]{2,1,0:T(8,128)(2,1)S(1)}, bf16[1,896,1024]{2,1,0:T(8,128)(2,1)}, u32[]{:S(2)}) copy-start(bf16[1,896,1024]{2,1,0:T(8,128)(2,1)} %param.11) | copy-start | bytes 5505028
  5.0 29.0 %all-to-all-start = ((bf16[32,8,896]{2,1,0:T(8,128)(2,1)}), bf16[32,8,896]{2,1,0:T(8,128)(2,1)S(1)}, u32[]{:S(2)}, u32[]{:S(2)}) async-start(bf16[32,8,896]{2,1,0:T(8,128)(2,1)} %fusion.5), calls=%async_computation | async-start | bytes 917504 | tf_op jit(solution)/shard_map/all_to_all | solution.py:76
  34.0 2.4 %copy-start.1 = (bf16[1024,896]{1,0:T(8,128)(2,1)S(1)}, bf16[1024,896]{1,0:T(8,128)(2,1)}, u32[]{:S(2)}) copy-start(bf16[1024,896]{1,0:T(8,128)(2,1)} %copy.47) | copy-start | bytes 5505028
where the time goes:
time: 114 us; the launch traced here: 113 us
  blocking collectives  67 us (59%)
  starting transfers between devices  12.6 us (11%)
  local copies, waits for them, and re-layouts  10.9 us (10%)
  waiting for transfers between devices  8.79 us (8%)
  other arithmetic  7.38 us (6%)
  matrix products  6.64 us (6%)
    all_to_all x1, blocking collectives, summed_on_arrival(): lax.all_to_all(blocks, axis, split_axis=0, concat_axis=0, tiled=True)  31.8 us
    all_to_all x1, blocking collectives, shards(): lax.all_to_all(column_rows.astype(jnp.bfloat16), 'expert', split_axis=1,...  23.5 us
    all_to_all x1, starting transfers between devices, shards(): lax.all_to_all(send_rows, 'expert', split_axis=0, concat_axis=1, tiled=True)  12.6 us
    all_to_all x1, blocking collectives, copy_for_each(): return lax.all_to_all(copies, axis, split_axis=0, concat_axis=0, tiled=True)  11.6 us
    all_to_all x1, waiting for transfers between devices, shards(): lax.all_to_all(send_rows, 'expert', split_axis=0, concat_axis=1, tiled=True)  8.79 us
    dot_general x1, local copies, waits for them, and re-layouts, shards(): jnp.einsum('erd,edf->erf', received, up_weight, preferred_element_type=jn...  3.84 us
    dot_general x1, local copies, waits for them, and re-layouts, shards(): jnp.einsum('erd,edf->erf', received, gate_weight, preferred_element_type=...  3.8 us
    unnamed x1, other arithmetic  3.41 us
  transfers between devices with their start and end apart: 1, of which 1 were waited for; matrix products, arithmetic and copies ran while one was open for 7% of the time, Pallas kernels for 0%

commit v1 on v0

--- a/solution.py
+++ b/solution.py
@@ -2,8 +2,18 @@
 import jax.numpy as jnp
 from jax import lax
 from jax.sharding import PartitionSpec as P
+from jax.lax import all_to_all, psum
 
 routed_scale = 2.5
+
+
+def treat_field_on(block_here, mesh_dim):
+    out_arr = psum(1, mesh_dim)
+    val2 = jnp.split(block_here, out_arr, axis=1)
+    item_now = jnp.stack(val2, axis=0)
+    mid_arr = all_to_all(item_now, mesh_dim, split_axis=0, concat_axis=0)
+    all_values = jnp.concatenate(mid_arr, axis=0)
+    return all_values
 
 
 def cut_along(array, dim, peers):
@@ -84,9 +94,7 @@
     column_rows = jnp.einsum(
         "erf,edf->erd", hidden, down_weight, preferred_element_type=jnp.float32
     )
-    returned = lax.all_to_all(
-        column_rows.astype(jnp.bfloat16), "expert", split_axis=1, concat_axis=0, tiled=True
-    ).astype(column_rows.dtype)
+    returned = treat_field_on(column_rows.astype(jnp.bfloat16), "expert").astype(column_rows.dtype)
     mixed = jnp.dot(
         combiner,
         returned.reshape(slot_count, narrow_width),

time: 114 us -> 109 us (0.956)
  other arithmetic: 7.38 us -> 4.1 us
  local copies, waits for them, and re-layouts: 10.9 us -> 9.28 us
    unnamed x1 -> x0, other arithmetic: 3.41 us -> none
    dot_general x1, matrix products: 0.76 us -> 2.37 us  [shards(): jnp.einsum('erd,edf->erf', received, gate_weight, preferred_element_type=...]
    dot_general x1, matrix products: 2.37 us -> 0.76 us  [shards(): jnp.einsum('erd,edf->erf', received, up_weight, preferred_element_type=jn...]
where the time goes in v1:
time: 109 us; the launch traced here: 108 us
  blocking collectives  66.8 us (61%)
  starting transfers between devices  12.6 us (12%)
  local copies, waits for them, and re-layouts  9.28 us (9%)
  waiting for transfers between devices  8.78 us (8%)
  matrix products  6.65 us (6%)
  other arithmetic  4.1 us (4%)
    all_to_all x1, blocking collectives, summed_on_arrival(): lax.all_to_all(blocks, axis, split_axis=0, concat_axis=0, tiled=True)  32.2 us
    all_to_all x1, blocking collectives, treat_field_on(): mid_arr = all_to_all(item_now, mesh_dim, split_axis=0, concat_axis=0)  23.4 us
    all_to_all x1, starting transfers between devices, shards(): lax.all_to_all(send_rows, 'expert', split_axis=0, concat_axis=1, tiled=True)  12.6 us
    all_to_all x1, blocking collectives, copy_for_each(): return lax.all_to_all(copies, axis, split_axis=0, concat_axis=0, tiled=True)  11.2 us
    all_to_all x1, waiting for transfers between devices, shards(): lax.all_to_all(send_rows, 'expert', split_axis=0, concat_axis=1, tiled=True)  8.78 us
    dot_general x1, local copies, waits for them, and re-layouts, shards(): jnp.einsum('erd,edf->erf', received, up_weight, preferred_element_type=jn...  3.83 us
    dot_general x1, local copies, waits for them, and re-layouts, shards(): jnp.einsum('erd,edf->erf', received, gate_weight, preferred_element_type=...  3.81 us
    dot_general x1, matrix products, shards(): jnp.einsum('erd,edf->erf', received, gate_weight, preferred_element_type=...  2.37 us
  transfers between devices with their start and end apart: 1, of which 1 were waited for; matrix products, arithmetic and copies ran while one was open for 7% of the time, Pallas kernels for 0%

profile of v1, /device:TPU:1, one launch (start us, length us, event | category | flops | bytes accessed | tf_op | source)
XLA Modules:
  0.0 108.5 jit_solution(7967980085066919876)
XLA Ops:
  0.0 0.0 copy-start
  0.0 0.8 fusion.17
  0.8 0.7 multiply_divide_fusion
  1.5 0.1 copy.28
  1.6 0.8 copy.26
  2.4 0.1 eq.30
  2.5 0.1 fusion.13
  2.6 0.2 reduce_window_sum.11
  2.7 0.2 select_reduce_fusion.1
  2.9 0.1 reduce_sum.48
  3.0 0.2 convert_reduce_fusion
  3.2 1.9 %fusion.5 = bf16[32,8,896]{2,1,0:T(8,128)(2,1)} fusion(bf16[16,7168]{1,0:T(8,128)(2,1)} %param.6, s32[]{:T(128)S(6)} %select_n.8, bf16[256,16]{0,1:T(8,128)(2,1)S(1)} %get-tuple-element.5), kind=kOutput, calls=%fused_computation.7 | convolution fusion | flops 7569408 | bytes 495620 | tf_op jit(solution)/shard_map/dot_general | solution.py:82
  5.0 12.6 %all-to-all-start = ((bf16[32,8,896]{2,1,0:T(8,128)(2,1)}), bf16[32,8,896]{2,1,0:T(8,128)(2,1)S(1)}, u32[]{:S(2)}, u32[]{:S(2)}) async-start(bf16[32,8,896]{2,1,0:T(8,128)(2,1)} %fusion.5), calls=%async_computation | async-start | bytes 917504 | tf_op jit(solution)/shard_map/all_to_all | solution.py:86
  17.6 3.8 %copy.35 = bf16[1024,896]{1,0:T(8,128)(2,1)} copy(bf16[1024,896]{0,1:T(8,128)(2,1)} %bitcast.177) | data formatting | bytes 3670016 | tf_op jit(solution)/shard_map/erd,edf->erf/dot_general | solution.py:87
  21.4 3.8 %copy.36 = bf16[1024,896]{1,0:T(8,128)(2,1)} copy(bf16[1024,896]{0,1:T(8,128)(2,1)} %bitcast.178) | data formatting | bytes 3670016 | tf_op jit(solution)/shard_map/erd,edf->erf/dot_general | solution.py:90
  25.3 8.8 %all-to-all-done = bf16[32,8,896]{2,1,0:T(8,128)(2,1)S(1)} async-done(((bf16[32,8,896]{2,1,0:T(8,128)(2,1)}), bf16[32,8,896]{2,1,0:T(8,128)(2,1)S(1)}, u32[]{:S(2)}, u32[]{:S(2)}) %all-to-all-start) | async-done | bytes 458784 | tf_op jit(solution)/shard_map/all_to_all | solution.py:86
  34.0 0.0 copy-start.1
  34.0 2.4 %convolution_bitcast_fusion.1 = f32[1,256,8,128]{3,1,2,0:T(8,128)S(1)} fusion(bf16[8,128,896]{2,1,0:T(8,128)(2,1)} %bitcast.176, bf16[32,8,896]{2,1,0:T(8,128)(2,1)S(1)} %all-to-all-done), kind=kOutput, calls=%fused_computation.4 | convolution fusion | flops 469762048 | bytes 3342336 | tf_op jit(solution)/shard_map/erd,edf->erf/dot_general | solution.py:87
  36.4 0.0 copy-done.1
  36.4 0.8 convolution_bitcast_fusion
  37.2 0.2 maximum_bitcast_fusion
  37.4 0.2 copy.31
  37.6 32.2 %all_to_all.24 = f32[8,2,256,128]{3,2,1,0:T(8,128)} all-to-all(f32[8,2,256,128]{3,2,1,0:T(8,128)S(1)} %copy.31), channel_id=1, replica_groups=mesh['expert'=32,'tensor'=8] {'tensor'}, dimensions={0} | all-to-all | bytes 4194304 | tf_op jit(solution)/shard_map/all_to_all | solution.py:27
  69.8 1.7 %reduce_sum.52 = f32[2,256,128]{2,1,0:T(8,128)S(1)} reduce(f32[8,2,256,128]{3,2,1,0:T(8,128)} %all_to_all.24, f32[]{:T(128)} %constant.6.clone.1), dimensions={0}, to_apply=%region_5.6 | reduce | flops 458752 | bytes 2359300 | tf_op jit(solution)/shard_map/reduce_sum | solution.py:28
  71.5 0.1 copy.33
  71.7 11.2 %all_to_all.25 = bf16[8,1,256,128]{2,3,1,0:T(8,128)(2,1)S(1)} all-to-all(bf16[8,1,256,128]{2,3,1,0:T(8,128)(2,1)S(1)} %broadcast_in_dim.22), channel_id=1, replica_groups=mesh['expert'=32,'tensor'=8] {'tensor'}, dimensions={0} | all-to-all | bytes 1048576 | tf_op jit(solution)/shard_map/all_to_all | solution.py:42
  82.9 0.0 copy-done
  82.9 0.8 fusion.6
  84.1 23.4 %all_to_all.26 = bf16[32,1,8,896]{3,2,1,0:T(8,128)(2,1)S(1)} all-to-all(bf16[32,1,8,896]{3,2,1,0:T(8,128)(2,1)S(1)} %constant_dynamic-update-slice_fusion), channel_id=1, replica_groups=mesh['expert'=32,'tensor'=8] {'expert'}, dimensions={0} | all-to-all | bytes 917504 | tf_op jit(solution)/shard_map/all_to_all | solution.py:14
  107.5 0.9 convolution_convert_fusion.1
  (35 shorter events, 0.4 us)
Async XLA Ops:
  0.0 82.9 %copy-start = (bf16[1,896,1024]{2,1,0:T(8,128)(2,1)S(1)}, bf16[1,896,1024]{2,1,0:T(8,128)(2,1)}, u32[]{:S(2)}) copy-start(bf16[1,896,1024]{2,1,0:T(8,128)(2,1)} %param.11) | copy-start | bytes 5505028
  5.0 29.0 %all-to-all-start = ((bf16[32,8,896]{2,1,0:T(8,128)(2,1)}), bf16[32,8,896]{2,1,0:T(8,128)(2,1)S(1)}, u32[]{:S(2)}, u32[]{:S(2)}) async-start(bf16[32,8,896]{2,1,0:T(8,128)(2,1)} %fusion.5), calls=%async_computation | async-start | bytes 917504 | tf_op jit(solution)/shard_map/all_to_all | solution.py:86
  34.0 2.4 %copy-start.1 = (bf16[1024,896]{1,0:T(8,128)(2,1)S(1)}, bf16[1024,896]{1,0:T(8,128)(2,1)}, u32[]{:S(2)}) copy-start(bf16[1024,896]{1,0:T(8,128)(2,1)} %copy.36) | copy-start | bytes 5505028
